TPU v7x, 32 devices: a whole 2x2x4 slice. The times are simulated.
32 devices in a mesh: groups: 2 (over x), gx: 16 (over z, y, core).
Axes of the slice: x: 2, y: 2, z: 4, core: 2. Of those that a mesh axis runs over, the one named last changes fastest.
Arguments:
- tokens: bfloat16 [512, 8192], P('groups', 'gx'), parts along dimension 0, may hold values from -6 to 6
- gate_weight: bfloat16 [8192, 14336], P(None, 'gx'), may hold values from -0.09375 to 0.09375
- up_weight: bfloat16 [8192, 14336], P(None, 'gx'), may hold values from -0.09375 to 0.09375
- down_weight: bfloat16 [14336, 8192], P('gx'), may hold values from -0.0625 to 0.0625
Outputs:
- mixed: bfloat16 [512, 8192], P('groups', 'gx'), parts along dimension 0
There are 2 independent parts, one for each index of `groups`. A program takes and returns all parts, laid end to end along the dimension named above; an argument that names none is the same for every part. Nothing has to cross between parts.
All inputs are finite; a program needn't handle non-finite values.
Results may differ from a plain program's by a relative error of at most 0.0049.
Values may be sent and summed in bfloat16 or wider, within the bound.
A program may use at most 128 MiB of HBM per device.

v0:
```python
import jax
import jax.numpy as jnp
from jax import lax
from jax.sharding import PartitionSpec as P


def on_device(tokens, gate_weight, up_weight, down_weight):
    whole = lax.all_gather(tokens, "gx", axis=1, tiled=True)
    gate = jnp.dot(whole, gate_weight, preferred_element_type=jnp.float32)
    up = jnp.dot(whole, up_weight, preferred_element_type=jnp.float32)
    hidden = (jax.nn.silu(gate) * up).astype(jnp.bfloat16)
    out_rows = lax.psum_scatter(
        lax.dot_general(
            down_weight, hidden, (((0,), (1,)), ((), ())), preferred_element_type=jnp.float32
        ),
        "gx",
        scatter_dimension=0,
        tiled=True,
    )
    return jnp.transpose(out_rows).astype(jnp.bfloat16)


def solution(mesh):
    return jax.shard_map(
        on_device,
        mesh=mesh,
        in_specs=(P("groups", "gx"), P(None, "gx"), P(None, "gx"), P("gx", None)),
        out_specs=P("groups", "gx"),
        check_vma=False,
    )
```

profile of v0, /device:TPU:0, one launch (start us, length us, event | category | flops | bytes accessed | tf_op | source)
XLA Modules:
  0.0 209.1 jit_solution(1416217101893573405)
XLA Ops:
  6.5 0.0 all-gather.2.cloned.1.call-start
  6.5 0.7 all-gather.2.cloned.1.call-update
  7.3 0.0 reduce-scatter.2.cloned.1.call-start
  7.3 57.4 %all-gather.2.cloned.1.call-done = bf16[256,8192]{1,0:T(8,128)(2,1)} async-done(((bf16[256,512]{1,0:T(8,128)(2,1)}), bf16[256,8192]{1,0:T(8,128)(2,1)}) %all-gather.2.cloned.1.call-update) | async-done | bytes 4194320 | tf_op jit(solution)/shard_map/all_gather | solution.py:8
  64.7 11.1 %fusion.2 = f32[256,896]{1,0:T(8,128)S(1)} fusion(bf16[256,8192]{1,0:T(8,128)(2,1)} %all-gather.2.cloned.1.call-done, bf16[8192,896]{1,0:T(8,128)(2,1)} %param.5), kind=kOutput, calls=%fused_computation.5 | convolution fusion | flops 3758096384 | bytes 19791872 | tf_op jit(solution)/shard_map/dot_general | solution.py:9
  75.8 22.7 %convolution_bitcast_fusion = f32[8192,256]{0,1:T(8,128)} fusion(bf16[896,8192]{1,0:T(8,128)(2,1)} %param.7, bf16[256,8192]{1,0:T(8,128)(2,1)} %all-gather.2.cloned.1.call-done, bf16[8192,896]{1,0:T(8,128)(2,1)} %param.6, f32[256,896]{1,0:T(8,128)S(1)} %fusion.2), kind=kOutput, calls=%fused_computation | convolution fusion | flops 7517569024 | bytes 42860544 | tf_op jit(solution)/shard_map/dot_general | solution.py:13
  98.5 0.0 reduce-scatter.2.cloned.1.call-update
  98.5 102.0 %reduce-scatter.2.cloned.1.call-done = f32[512,256]{0,1:T(8,128)} async-done(((f32[8192,256]{0,1:T(8,128)}), f32[512,256]{0,1:T(8,128)}) %reduce-scatter.2.cloned.1.call-update) | async-done | bytes 524304 | tf_op jit(solution)/shard_map/reduce_scatter | solution.py:12
  200.5 1.8 convert_bitcast_fusion
Async XLA Ops:
  6.5 58.2 %all-gather.2.cloned.1.call-start = ((), (), s32[]{:S(2)}) async-start(), calls=%async_computation.1 | async-start | bytes 4456448 | tf_op jit(solution)/shard_map/all_gather | solution.py:8
  7.3 193.2 %reduce-scatter.2.cloned.1.call-start = ((), (), s32[]{:S(2)}) async-start(), calls=%async_computation.2 | async-start | bytes 8912896 | tf_op jit(solution)/shard_map/reduce_scatter | solution.py:12
Sparse Core Ops, SparseCore 0:
  9.5 55.1 all-gather.1
  98.6 101.7 reduce-scatter.1
where the time goes:
time: 209 us
  waiting for transfers between devices  160 us (77%)
  matrix products  33.8 us (16%)
  between operations  13.4 us (6%)
    reduce_scatter x1, waiting for transfers between devices, on_device(): lax.psum_scatter(lax.dot_general(down_weight, hidden, (((0,), (1,)), ((),...  102 us
    all_gather x1, waiting for transfers between devices, on_device(): whole = lax.all_gather(tokens, 'gx', axis=1, tiled=True)  57.4 us
    dot_general x1, matrix products, on_device(): lax.dot_general(down_weight, hidden, (((0,), (1,)), ((), ())), preferred_...  22.7 us
    dot_general x1, matrix products, on_device(): gate = jnp.dot(whole, gate_weight, preferred_element_type=jnp.float32)  11.1 us
  transfers between devices with their start and end apart: 2, of which 2 were waited for; matrix products, arithmetic and copies ran while one was open for 0% of the time, Pallas kernels for 0%

commit v1 on v0

v1 whole, which is shorter than its diff:
```python
import functools

import jax
import jax.numpy as jnp
from jax import lax
from jax.experimental import pallas as pl
from jax.experimental.pallas import tpu as pltpu
from jax.sharding import PartitionSpec as P

MESH = pl.DeviceIdType.MESH
VMEM_LIMIT = 67043328


def kernel(
    n, width, tok_hbm, gate_hbm, up_hbm, down_hbm, out_ref,
    tok, wg, wu, wd, acc_g, acc_u, hid, own, sout, sin, rin, rout,
    tok_sem, w_sem, d_sem, ag_send, ag_recv, sib_send, sib_recv,
    pair_send, pair_recv, rs_send, rs_recv,
):
    half = n // 2
    token_rows, block = tok_hbm.shape
    hrows = token_rows // 2
    long = n // width
    me = lax.axis_index("gx")
    core = lax.rem(me, 2)
    chip = me // 2
    z = chip // width
    y = chip - z * width
    r = z + y * (n - 1 - 2 * z)

    def device_at(pos, c):
        pos = lax.rem(pos + n, n)
        yy = pos // long
        zz = pos + yy * (n - 1 - 2 * pos)
        return (zz * width + yy) * 2 + c

    sib = me + 1 - 2 * core
    target = (device_at(r + 1, core), device_at(r - 1, core))

    def rows(h):
        return pl.ds(h * hrows, hrows)

    def slot(k, d, cr):
        if k == 0:
            return cr
        if k < half:
            return 2 + (k - 1) * 4 + d * 2 + cr
        return 2 + (half - 1) * 4 + cr

    def step_slots(k):
        dirs = (0, 1) if 0 < k < half else (0,)
        return [(d, cr, slot(k, d, cr)) for d in dirs for cr in (0, 1)]

    sends = []

    def remote(src, dst, s_sem, r_sem, dev):
        return pltpu.make_async_remote_copy(
            src_ref=src, dst_ref=dst, send_sem=s_sem, recv_sem=r_sem,
            device_id={"gx": dev}, device_id_type=MESH,
        )

    def send(*args):
        copy = remote(*args)
        copy.start()
        sends.append(copy)

    def weight_copies(s, dev):
        part = pl.ds(pl.multiple_of(dev * block, block), block)
        return (
            pltpu.make_async_copy(gate_hbm.at[part], wg.at[s], w_sem.at[0, s]),
            pltpu.make_async_copy(up_hbm.at[part], wu.at[s], w_sem.at[1, s]),
        )

    def start_weights(k):
        for d, cr, s in step_slots(k):
            pos = r - k if d == 0 else r + k
            c = core if cr == 0 else 1 - core
            for copy in weight_copies(s, device_at(pos, c)):
                copy.start()

    def down_copy(q, cr):
        c = core if cr == 0 else 1 - core
        dev = device_at(r + q, c)
        part = pl.ds(pl.multiple_of(dev * block, block), block)
        s = 2 * q + cr
        return pltpu.make_async_copy(down_hbm.at[:, part], wd.at[s], d_sem.at[s])

    def add_block(s):
        for copy in weight_copies(s, 0):
            copy.wait()
        x = tok[s]
        acc_g[...] += jnp.dot(x, wg[s], preferred_element_type=jnp.float32)
        acc_u[...] += jnp.dot(x, wu[s], preferred_element_type=jnp.float32)

    def add_step(k, cr):
        slots = [s for _, c, s in step_slots(k) if c == cr]
        if len(slots) == 1:
            add_block(slots[0])
        else:
            @pl.loop(0, 2)
            def _(i):
                add_block(slots[0] + 2 * i)

    first = pltpu.make_async_copy(tok_hbm, tok.at[0], tok_sem)
    first.start()
    barrier = pltpu.get_barrier_semaphore()
    for dev in (*target, sib):
        pl.semaphore_signal(barrier, inc=1, device_id={"gx": dev}, device_id_type=MESH)
    start_weights(0)
    start_weights(1)
    acc_g[...] = jnp.zeros_like(acc_g)
    acc_u[...] = jnp.zeros_like(acc_u)
    first.wait()
    pl.semaphore_wait(barrier, 3)

    def ring_copy(k, d, h):
        src = tok.at[slot(k - 1, d, 0), rows(h)]
        dst = tok.at[slot(k, d, 0), rows(h)]
        return src, dst, ag_send.at[d, k, h], ag_recv.at[d, k, h], target[d]

    def pair_copy(k, d, h):
        src = tok.at[slot(k, d, 0), rows(h)]
        dst = tok.at[slot(k, d, 1), rows(h)]
        return src, dst, sib_send.at[d, k, h], sib_recv.at[d, k, h], sib

    for part in (0, 1):
        for d in (0, 1):
            send(*ring_copy(1, d, d if part == 0 else 1 - d))
    for h in (0, 1):
        send(*pair_copy(0, 0, h))
    for k in range(1, half + 1):
        if k < half:
            start_weights(k + 1)
        qs = [q for q in range(n) if q % half == k - 1]
        for q in qs:
            for cr in (0, 1):
                down_copy(q, cr).start()
        for part in (0, 1):
            for d in (0, 1):
                h = d if part == 0 else 1 - d
                if k == half and part == 1:
                    continue
                remote(*ring_copy(k, d, h)).wait_recv()
                if k + 1 < half or (k + 1 == half and part == 0):
                    send(*ring_copy(k + 1, d, h))
                send(*pair_copy(k, d, h))
            if part == 1:
                for d in (0, 1) if k > 1 else (0,):
                    for h in (0, 1):
                        remote(*pair_copy(k - 1, d, h)).wait_recv()
            add_step(k - 1, part)
    add_step(half, 0)
    for d in (0, 1):
        remote(*pair_copy(half, d, d)).wait_recv()
    add_step(half, 1)

    gate = acc_g[...]
    hid[...] = (gate / (1.0 + jnp.exp(-gate)) * acc_u[...]).astype(hid.dtype)

    def partial(q, cr):
        down_copy(q, cr).wait()
        return jnp.dot(hid[...], wd[2 * q + cr], preferred_element_type=jnp.float32)

    def sib_copy(q):
        return sout.at[q], sin.at[q], pair_send.at[q], pair_recv.at[q], sib

    def for_sib(q):
        sout[q] = partial(q, 1).astype(sout.dtype)
        send(*sib_copy(q))

    def for_own(q):
        own[q] = partial(q, 0)

    seen = set()

    def pair_sum(q, h):
        if q not in seen:
            seen.add(q)
            remote(*sib_copy(q)).wait_recv()
        return own[q, rows(h)] + sin[q, rows(h)].astype(jnp.float32)

    def sum_copy(o, d, h):
        return (rout.at[d, o - 1, h], rin.at[d, o - 1, h],
                rs_send.at[d, o - 1, h], rs_recv.at[d, o - 1, h], target[d])

    def arrived(o, d, h):
        remote(*sum_copy(o + 1, d, h)).wait_recv()
        return rin[d, o, h].astype(jnp.float32)

    def dest(o, d):
        return o % n if d == 0 else (n - o) % n

    def group(o):
        return sorted({dest(o, 0), dest(o, 1)})

    for o in (half, half - 1):
        for q in group(o):
            for_sib(q)
    for_own(half)
    for d in (0, 1):
        rout[d, half - 1, d] = pair_sum(half, d).astype(rout.dtype)
        send(*sum_copy(half, d, d))
    for q in group(half - 1):
        for_own(q)
    for o in range(half - 1, 0, -1):
        for part in (0, 1):
            for d in (0, 1):
                h = 1 - d if part == 0 else d
                total = pair_sum(dest(o, d), h)
                if part == 1 or o < half - 1:
                    total = total + arrived(o, d, h)
                rout[d, o - 1, h] = total.astype(rout.dtype)
                send(*sum_copy(o, d, h))
            if part == 0:
                for q in group(o - 1):
                    for_sib(q)
                for q in group(o - 1):
                    for_own(q)
    for d in (0, 1):
        own[0, rows(1 - d)] = pair_sum(0, 1 - d) + arrived(0, d, 1 - d)
    for d in (0, 1):
        out_ref[rows(d)] = (own[0, rows(d)] + arrived(0, d, d)).astype(out_ref.dtype)
    for copy in sends:
        copy.wait_send()


def on_device(n, width, tokens, gate_weight, up_weight, down_weight):
    token_rows, block = tokens.shape
    hidden = gate_weight.shape[1]
    half = n // 2
    slots = 2 * n
    hrows = token_rows // 2
    bf16, f32 = jnp.bfloat16, jnp.float32
    dma = pltpu.SemaphoreType.DMA
    ring = (2, half + 1, 2)
    return pl.pallas_call(
        functools.partial(kernel, n, width),
        out_shape=jax.ShapeDtypeStruct((token_rows, block), bf16),
        in_specs=[pl.BlockSpec(memory_space=pl.ANY)] * 4,
        out_specs=pl.BlockSpec(memory_space=pltpu.VMEM),
        scratch_shapes=[
            pltpu.VMEM((slots, token_rows, block), bf16),
            pltpu.VMEM((slots, block, hidden), bf16),
            pltpu.VMEM((slots, block, hidden), bf16),
            pltpu.VMEM((slots, hidden, block), bf16),
            pltpu.VMEM((token_rows, hidden), f32),
            pltpu.VMEM((token_rows, hidden), f32),
            pltpu.VMEM((token_rows, hidden), bf16),
            pltpu.VMEM((n, token_rows, block), f32),
            pltpu.VMEM((n, token_rows, block), bf16),
            pltpu.VMEM((n, token_rows, block), bf16),
            pltpu.VMEM((2, half, 2, hrows, block), bf16),
            pltpu.VMEM((2, half, 2, hrows, block), bf16),
            dma(()), dma((2, slots)), dma((slots,)),
            dma(ring), dma(ring), dma(ring), dma(ring),
            dma((n,)), dma((n,)), dma((2, half, 2)), dma((2, half, 2)),
        ],
        compiler_params=pltpu.CompilerParams(
            collective_id=0, has_side_effects=True, vmem_limit_bytes=VMEM_LIMIT
        ),
    )(tokens, gate_weight, up_weight, down_weight)


def solution(mesh):
    n = mesh.shape["gx"] // 2
    spots = {tuple(getattr(dev, "coords", (0, 0, 0)))[:2] for dev in mesh.devices[0]}
    width = len(spots) if len(spots) in (1, 2) else 1
    return jax.shard_map(
        functools.partial(on_device, n, width),
        mesh=mesh,
        in_specs=(P("groups", "gx"), P(None, "gx"), P(None, "gx"), P("gx", None)),
        out_specs=P("groups", "gx"),
        check_vma=False,
    )
```

time: 209 us -> 57.4 us (0.27)
  waiting for transfers between devices: 160 us -> 0 us
  Pallas kernels: 0 us -> 55.5 us
  matrix products: 33.8 us -> 0 us
  between operations: 13.4 us -> 0.01 us
    reduce_scatter x1 -> x0, waiting for transfers between devices: 102 us -> none  [on_device(): lax.psum_scatter(lax.dot_general(down_weight, hidden, (((0,), (1,)), ((),...]
    all_gather x1 -> x0, waiting for transfers between devices: 57.4 us -> none  [on_device(): whole = lax.all_gather(tokens, 'gx', axis=1, tiled=True)]
    pallas_call x0 -> x1, Pallas kernels: none -> 55.5 us  [on_device(): pl.pallas_call(functools.partial(kernel, n, width), out_shape=jax.ShapeDt...]
    dot_general x2 -> x0, matrix products: 33.8 us -> none  [the longest x1 22.7 us: on_device(): lax.dot_general(down_weight, hidden, (((0,), (1,)), ((), ())), preferred_...]
  transfers between devices with their start and end apart: 2 -> 0, of which waited for: 2 -> 0; matrix products, arithmetic and copies ran while one was open for 0% -> 0% of each run, Pallas kernels for 0% -> 0%
where the time goes in v1:
time: 57.4 us; the launch traced here: 57.2 us
  Pallas kernels  55.5 us (97%)
  local copies, waits for them, and re-layouts  1.67 us (3%)
    pallas_call x1, Pallas kernels, on_device(): pl.pallas_call(functools.partial(kernel, n, width), out_shape=jax.ShapeDt...  55.5 us
    unnamed x1, local copies, waits for them, and re-layouts  1.67 us

profile of v1, /device:TPU:0, one launch (start us, length us, event | category | flops | bytes accessed | tf_op | source)
XLA Modules:
  0.0 57.2 jit_solution(12597451209138927560)
XLA Ops:
  0.0 55.5 %shard_map.46 = bf16[256,512]{1,0:T(8,128)(2,1)} custom-call(bf16[256,512]{1,0:T(8,128)(2,1)} %tok_hbm.1, bf16[8192,896]{1,0:T(8,128)(2,1)} %gate_hbm.1, bf16[8192,896]{1,0:T(8,128)(2,1)} %up_hbm.1, bf16[896,8192]{1,0:T(8,128)(2,1)} %down_hbm.1), custom_call_target="tpu_custom_call" | custom-call | tf_op jit(solution)/shard_map/pallas_call | solution.py:236
  55.5 1.7 %copy.6 = bf16[256,512]{1,0:T(8,128)(2,1)} copy(bf16[256,512]{1,0:T(8,128)(2,1)} %shard_map.46) | data formatting | bytes 524288

commit v2 on v1

v2 whole, which is shorter than its diff:
```python
import functools

import jax
import jax.numpy as jnp
from jax import lax
from jax.experimental import pallas as pl
from jax.experimental.pallas import tpu as pltpu
from jax.sharding import PartitionSpec as P

MESH = pl.DeviceIdType.MESH
VMEM_LIMIT = 67043328


def kernel(
    n, width, tok_hbm, gate_hbm, up_hbm, down_hbm, out_ref,
    tok, wg, wu, wd, acc_g, acc_u, hid, own, sout, sin, rin, rout,
    tok_sem, w_sem, d_sem, ag_send, ag_recv, sib_send, sib_recv,
    pair_send, pair_recv, rs_send, rs_recv,
):
    half = n // 2
    token_rows, block = tok_hbm.shape
    prow = token_rows // 4
    long = n // width
    me = lax.axis_index("gx")
    core = lax.rem(me, 2)
    chip = me // 2
    z = chip // width
    y = chip - z * width
    r = z + y * (n - 1 - 2 * z)

    def device_at(pos, c):
        pos = lax.rem(pos + n, n)
        yy = pos // long
        zz = pos + yy * (n - 1 - 2 * pos)
        return (zz * width + yy) * 2 + c

    sib = me + 1 - 2 * core
    target = (device_at(r + 1, core), device_at(r - 1, core))

    def rows(p):
        return pl.ds(p * prow, prow)

    def span(ph):
        return pl.ds(0, 4 * prow) if ph is None else pl.ds(2 * ph * prow, 2 * prow)

    def piece(ph, part, d):
        return 2 * ph + (d if part == 0 else 1 - d)

    def slot(k, d, cr):
        if k == 0:
            return cr
        if k < half:
            return 2 + (k - 1) * 4 + d * 2 + cr
        return 2 + (half - 1) * 4 + cr

    def step_slots(k):
        dirs = (0, 1) if 0 < k < half else (0,)
        return [(d, cr, slot(k, d, cr)) for d in dirs for cr in (0, 1)]

    sends = []

    def remote(src, dst, s_sem, r_sem, dev):
        return pltpu.make_async_remote_copy(
            src_ref=src, dst_ref=dst, send_sem=s_sem, recv_sem=r_sem,
            device_id={"gx": dev}, device_id_type=MESH,
        )

    def send(*args):
        copy = remote(*args)
        copy.start()
        sends.append(copy)

    def weight_copies(s, dev):
        part = pl.ds(pl.multiple_of(dev * block, block), block)
        return (
            pltpu.make_async_copy(gate_hbm.at[part], wg.at[s], w_sem.at[0, s]),
            pltpu.make_async_copy(up_hbm.at[part], wu.at[s], w_sem.at[1, s]),
        )

    def start_weights(k):
        for d, cr, s in step_slots(k):
            pos = r - k if d == 0 else r + k
            c = core if cr == 0 else 1 - core
            for copy in weight_copies(s, device_at(pos, c)):
                copy.start()

    def down_copy(q, cr):
        c = core if cr == 0 else 1 - core
        dev = device_at(r + q, c)
        part = pl.ds(pl.multiple_of(dev * block, block), block)
        s = 2 * q + cr
        return pltpu.make_async_copy(down_hbm.at[:, part], wd.at[s], d_sem.at[s])

    def add_block(s, ph, fresh):
        if fresh:
            for copy in weight_copies(s, 0):
                copy.wait()
        at = span(ph)
        x = tok[s, at]
        acc_g[at] += jnp.dot(x, wg[s], preferred_element_type=jnp.float32)
        acc_u[at] += jnp.dot(x, wu[s], preferred_element_type=jnp.float32)

    first = pltpu.make_async_copy(tok_hbm, tok.at[0], tok_sem)
    first.start()
    barrier = pltpu.get_barrier_semaphore()
    for dev in (*target, sib):
        pl.semaphore_signal(barrier, inc=1, device_id={"gx": dev}, device_id_type=MESH)
    start_weights(0)
    start_weights(1)
    first.wait()
    pl.semaphore_wait(barrier, 3)

    def ring_copy(k, d, h):
        src = tok.at[slot(k - 1, d, 0), rows(h)]
        dst = tok.at[slot(k, d, 0), rows(h)]
        return src, dst, ag_send.at[d, k, h], ag_recv.at[d, k, h], target[d]

    def pair_copy(k, d, h):
        src = tok.at[slot(k, d, 0), rows(h)]
        dst = tok.at[slot(k, d, 1), rows(h)]
        return src, dst, sib_send.at[d, k, h], sib_recv.at[d, k, h], sib

    def move(ph, part, k):
        for d in (0, 1):
            p = piece(ph, part, d)
            if k > 1:
                remote(*ring_copy(k - 1, d, p)).wait_recv()
            if k < half or (k == half and part == 0):
                send(*ring_copy(k, d, p))
            if k > 1:
                send(*pair_copy(k - 1, d, p))

    came = set()

    def add_step(k, cr, ph):
        if cr == 1:
            phases = (0, 1) if ph is None else (ph,)
            for d, c, s in step_slots(k):
                for p in [2 * a + b for a in phases for b in (0, 1)]:
                    if c == 1:
                        way = p % 2 if k == half else d
                        remote(*pair_copy(k, way, p)).wait_recv()
        slots = [s for _, c, s in step_slots(k) if c == cr]
        fresh = (k, cr) not in came
        came.add((k, cr))
        if len(slots) == 1:
            add_block(slots[0], ph, fresh)
        else:
            @pl.loop(0, 2)
            def _(i):
                add_block(slots[0] + 2 * i, ph, fresh)

    def activate(ph):
        at = span(ph)
        gate = acc_g[at]
        hid[at] = (gate / (1.0 + jnp.exp(-gate)) * acc_u[at]).astype(hid.dtype)

    loaded = set()

    def partial(q, cr, ph):
        if (q, cr) not in loaded:
            loaded.add((q, cr))
            down_copy(q, cr).wait()
        return jnp.dot(hid[span(ph)], wd[2 * q + cr], preferred_element_type=jnp.float32)

    def sib_copy(q, ph):
        at = span(ph)
        return sout.at[q, at], sin.at[q, at], pair_send.at[q, ph], pair_recv.at[q, ph], sib

    def for_sib(q, ph):
        sout[q, span(ph)] = partial(q, 1, ph).astype(sout.dtype)
        send(*sib_copy(q, ph))

    def for_own(q, ph):
        own[q, span(ph)] = partial(q, 0, ph)

    seen = set()

    def pair_sum(q, p):
        if (q, p // 2) not in seen:
            seen.add((q, p // 2))
            remote(*sib_copy(q, p // 2)).wait_recv()
        return own[q, rows(p)] + sin[q, rows(p)].astype(jnp.float32)

    def sum_copy(o, d, p):
        return (rout.at[d, o - 1, p], rin.at[d, o - 1, p],
                rs_send.at[d, o - 1, p], rs_recv.at[d, o - 1, p], target[d])

    def arrived(o, d, p):
        remote(*sum_copy(o + 1, d, p)).wait_recv()
        return rin[d, o, p].astype(jnp.float32)

    def dest(o, d):
        return o % n if d == 0 else (n - o) % n

    def group(o):
        return sorted({dest(o, 0), dest(o, 1)})

    def project(o, ph):
        for q in group(o):
            for_sib(q, ph)
        for q in group(o):
            for_own(q, ph)

    def pass_sum(ph, part, o):
        for d in (0, 1):
            p = piece(ph, part, d)
            total = pair_sum(dest(o, d), p)
            if o < half - 1 or (o == half - 1 and part == 0):
                total = total + arrived(o, d, p)
            rout[d, o - 1, p] = total.astype(rout.dtype)
            send(*sum_copy(o, d, p))

    def finish(ph):
        for d in (0, 1):
            p = piece(ph, 1, d)
            own[0, rows(p)] = pair_sum(0, p) + arrived(0, d, p)
        for d in (0, 1):
            p = piece(ph, 0, d)
            out_ref[rows(p)] = (own[0, rows(p)] + arrived(0, d, p)).astype(out_ref.dtype)

    def start_down(os):
        for q in [q for o in os for q in group(o)]:
            for cr in (0, 1):
                down_copy(q, cr).start()

    spare = [(part, k) for k in range(1, half) for part in (0, 1)] + [(0, half)]
    for k in range(1, half):
        move(0, 0, k)
        move(0, 1, k)
        if k == 1:
            for p in range(4):
                send(*pair_copy(0, 0, p))
        move(1, *spare[k - 1])
        start_weights(k + 1)
        if k == 1:
            acc_g[...] = jnp.zeros_like(acc_g)
            acc_u[...] = jnp.zeros_like(acc_u)
            add_step(0, 0, None)
            add_step(0, 1, None)
        else:
            add_step(k - 1, 0, 0)
            add_step(k - 1, 1, 0)
            start_down([o for o in range(half, -1, -1) if o % (half - 2) == k % (half - 2)])
    move(0, 0, half)
    move(0, 1, half)
    rest = spare[half - 1:] + [(1, half), (0, half + 1)]
    move(1, *rest.pop(0))
    add_step(half - 1, 0, 0)
    move(1, *rest.pop(0))
    add_step(half - 1, 1, 0)
    done = 0
    move(0, 0, half + 1)
    add_step(half, 0, 0)
    if half > 3:
        add_step(1, 0, 1)
        done = 1
    move(1, *rest.pop(0))
    add_step(half, 1, 0)
    activate(0)
    for o in (half, half - 1):
        for q in group(o):
            for_sib(q, 0)
    move(1, *rest.pop(0))
    for_own(half, 0)
    pass_sum(0, 0, half)
    for q in group(half - 1):
        for_own(q, 0)
    pass_sum(0, 1, half - 1)
    if done:
        add_step(1, 1, 1)
    k = 1 + done
    while rest:
        part, hops = rest.pop(0)
        last = hops - 2 if part == 1 else k
        while k <= last and part == 1:
            add_step(k, 0, 1)
            add_step(k, 1, 1)
            k += 1
        if not rest:
            project(half - 2, 0)
            while k < half:
                add_step(k, 0, 1)
                add_step(k, 1, 1)
                k += 1
        move(1, part, hops)
    add_step(half, 0, 1)
    pass_sum(0, 0, half - 1)
    add_step(half, 1, 1)
    activate(1)
    pass_sum(0, 1, half - 2)
    project(half, 1)
    pass_sum(1, 0, half)
    project(half - 1, 1)
    pass_sum(1, 1, half - 1)
    for o in range(half - 2, 0, -1):
        project(o - 1, 0)
        pass_sum(0, 0, o)
        if o > 1:
            pass_sum(0, 1, o - 1)
        project(o, 1)
        pass_sum(1, 0, o + 1)
        pass_sum(1, 1, o)
    finish(0)
    project(0, 1)
    pass_sum(1, 0, 1)
    finish(1)
    for copy in sends:
        copy.wait_send()


def on_device(n, width, tokens, gate_weight, up_weight, down_weight):
    token_rows, block = tokens.shape
    hidden = gate_weight.shape[1]
    half = n // 2
    slots = 2 * n
    prow = token_rows // 4
    bf16, f32 = jnp.bfloat16, jnp.float32
    dma = pltpu.SemaphoreType.DMA
    ring = (2, half + 1, 4)
    return pl.pallas_call(
        functools.partial(kernel, n, width),
        out_shape=jax.ShapeDtypeStruct((token_rows, block), bf16),
        in_specs=[pl.BlockSpec(memory_space=pl.ANY)] * 4,
        out_specs=pl.BlockSpec(memory_space=pltpu.VMEM),
        scratch_shapes=[
            pltpu.VMEM((slots, token_rows, block), bf16),
            pltpu.VMEM((slots, block, hidden), bf16),
            pltpu.VMEM((slots, block, hidden), bf16),
            pltpu.VMEM((slots, hidden, block), bf16),
            pltpu.VMEM((token_rows, hidden), f32),
            pltpu.VMEM((token_rows, hidden), f32),
            pltpu.VMEM((token_rows, hidden), bf16),
            pltpu.VMEM((n, token_rows, block), f32),
            pltpu.VMEM((n, token_rows, block), bf16),
            pltpu.VMEM((n, token_rows, block), bf16),
            pltpu.VMEM((2, half, 4, prow, block), bf16),
            pltpu.VMEM((2, half, 4, prow, block), bf16),
            dma(()), dma((2, slots)), dma((slots,)),
            dma(ring), dma(ring), dma(ring), dma(ring),
            dma((n, 2)), dma((n, 2)), dma((2, half, 4)), dma((2, half, 4)),
        ],
        compiler_params=pltpu.CompilerParams(
            collective_id=0, has_side_effects=True, vmem_limit_bytes=VMEM_LIMIT
        ),
    )(tokens, gate_weight, up_weight, down_weight)


def solution(mesh):
    n = mesh.shape["gx"] // 2
    spots = {tuple(getattr(dev, "coords", (0, 0, 0)))[:2] for dev in mesh.devices[0]}
    width = len(spots) if len(spots) in (1, 2) else 1
    return jax.shard_map(
        functools.partial(on_device, n, width),
        mesh=mesh,
        in_specs=(P("groups", "gx"), P(None, "gx"), P(None, "gx"), P("gx", None)),
        out_specs=P("groups", "gx"),
        check_vma=False,
    )
```

time: 57.4 us -> 56.5 us (0.984)
  Pallas kernels: 55.5 us -> 54.6 us
    pallas_call x1, Pallas kernels: 55.5 us -> 54.6 us  [on_device(): pl.pallas_call(functools.partial(kernel, n, width), out_shape=jax.ShapeDt...]
where the time goes in v2:
time: 56.5 us; the launch traced here: 56.3 us
  Pallas kernels  54.6 us (97%)
  local copies, waits for them, and re-layouts  1.67 us (3%)
    pallas_call x1, Pallas kernels, on_device(): pl.pallas_call(functools.partial(kernel, n, width), out_shape=jax.ShapeDt...  54.6 us
    unnamed x1, local copies, waits for them, and re-layouts  1.67 us

profile of v2, /device:TPU:0, one launch (start us, length us, event | category | flops | bytes accessed | tf_op | source)
XLA Modules:
  0.0 56.3 jit_solution(17331640321645720051)
XLA Ops:
  0.0 54.6 %shard_map.46 = bf16[256,512]{1,0:T(8,128)(2,1)} custom-call(bf16[256,512]{1,0:T(8,128)(2,1)} %tok_hbm.1, bf16[8192,896]{1,0:T(8,128)(2,1)} %gate_hbm.1, bf16[8192,896]{1,0:T(8,128)(2,1)} %up_hbm.1, bf16[896,8192]{1,0:T(8,128)(2,1)} %down_hbm.1), custom_call_target="tpu_custom_call" | custom-call | tf_op jit(solution)/shard_map/pallas_call | solution.py:321
  54.6 1.7 %copy.6 = bf16[256,512]{1,0:T(8,128)(2,1)} copy(bf16[256,512]{1,0:T(8,128)(2,1)} %shard_map.46) | data formatting | bytes 524288
